TPU v7x, 32 devices: a whole 2x2x4 slice. The times are simulated.
32 devices in a mesh: expert: 8 (over z, x), dp: 4 (over y, core).
Axes of the slice: x: 2, y: 2, z: 4, core: 2. Of those that a mesh axis runs over, the one named last changes fastest.
Arguments:
- tokens: bfloat16 [8192, 2048], P(('expert', 'dp')), may hold values from -256 to 256
- routes: int32 [8192, 2], P(('expert', 'dp')), may hold values from 0 to 31, all different within a row
- priority: int32 [32, 256], P(('expert', 'dp')), may hold values from 0 to 255, each once within a row
- router: bfloat16 [2048, 32], replicated, may hold values from -3 to 3
- w_in: bfloat16 [32, 2048, 1024], P(('expert', 'dp')), may hold values from -0.125 to 0.125
- w_out: bfloat16 [32, 2048, 1024], P(('expert', 'dp')), may hold values from -0.1875 to 0.1875
Outputs:
- mixed: bfloat16 [8192, 2048], P(('expert', 'dp'))
- aux_loss: float32 [], replicated
Inputs may be any that keep to these rules, and one draw needn't show every extreme that they name: `routes`: a token's two experts differ; every expert is named by some token. `priority`: each group's 256 tokens hold every rank once.
All inputs are finite; a program needn't handle non-finite values.
Results may differ from a plain program's by a relative error of at most 0.0014.
The roundings to bfloat16 on the way count: a program that leaves them out, or rounds other values in their place, can miss the bound.
Values may be sent and summed in bfloat16 or wider, within the bound.
A program may use at most 64 MiB of HBM per device.

v0:
```python
import jax
import jax.numpy as jnp
from jax import lax
from jax.sharding import PartitionSpec as P


def send_rows(outgoing):
    column = lax.all_to_all(outgoing, "dp", split_axis=1, concat_axis=1, tiled=True)
    arrived = lax.all_to_all(column, "expert", split_axis=0, concat_axis=0, tiled=True)
    return arrived


def return_rows(produced):
    column = lax.all_to_all(produced, "expert", split_axis=0, concat_axis=0, tiled=True)
    returned = lax.all_to_all(column, "dp", split_axis=1, concat_axis=1, tiled=True)
    return returned


def shards(tokens, routes, priority, router, w_in, w_out):
    group_rows = tokens.shape[0]
    width = tokens.shape[1]
    experts = router.shape[1]
    slot_cap = 4 * group_rows // experts
    owner_count = lax.axis_size("expert")
    column_count = lax.axis_size("dp")
    logits = jnp.dot(tokens, router, preferred_element_type=jnp.float32)
    probs = jax.nn.softmax(logits, axis=-1)
    expert_grid = lax.broadcasted_iota(jnp.int32, (group_rows, experts), 1)
    first = routes[:, 0]
    second = routes[:, 1]
    first_hot = (expert_grid == first[:, None]).astype(jnp.float32)
    second_hot = (expert_grid == second[:, None]).astype(jnp.float32)
    logit_first = jnp.sum(logits * first_hot, axis=1)
    logit_second = jnp.sum(logits * second_hot, axis=1)
    gate_first = jax.nn.sigmoid(logit_first - logit_second).astype(jnp.bfloat16)
    gate_second = jax.nn.sigmoid(logit_second - logit_first).astype(jnp.bfloat16)
    ranks = priority[0]
    earlier = (ranks[None, :] < ranks[:, None]).astype(jnp.bfloat16)
    before_first = jnp.dot(
        earlier, first_hot.astype(jnp.bfloat16), preferred_element_type=jnp.float32
    )
    before_second = jnp.dot(
        earlier, second_hot.astype(jnp.bfloat16), preferred_element_type=jnp.float32
    )
    first_load = jnp.sum(first_hot, axis=0)
    pos_first = jnp.sum(before_first * first_hot, axis=1).astype(jnp.int32)
    pos_second = jnp.sum((before_second + first_load[None, :]) * second_hot, axis=1).astype(
        jnp.int32
    )
    slot_first = jnp.where(pos_first < slot_cap, first * slot_cap + pos_first, -1)
    slot_second = jnp.where(pos_second < slot_cap, second * slot_cap + pos_second, -1)
    slot_grid = lax.broadcasted_iota(jnp.int32, (experts * slot_cap, group_rows), 0)
    dispatch = ((slot_grid == slot_first[None, :]) | (slot_grid == slot_second[None, :])).astype(
        jnp.bfloat16
    )
    outgoing = jnp.dot(dispatch, tokens, preferred_element_type=jnp.float32).astype(jnp.bfloat16)
    outgoing = outgoing.reshape(owner_count, column_count, slot_cap, width)
    arrived = send_rows(outgoing)
    expert_rows = arrived.reshape(experts * slot_cap, width)
    hidden = jax.nn.relu(jnp.dot(expert_rows, w_in[0], preferred_element_type=jnp.float32)).astype(
        jnp.bfloat16
    )
    produced = lax.dot_general(
        hidden, w_out[0], (((1,), (1,)), ((), ())), preferred_element_type=jnp.float32
    ).astype(jnp.bfloat16)
    returned = return_rows(produced.reshape(owner_count, column_count, slot_cap, width))
    returned = returned.reshape(experts * slot_cap, width)
    token_grid = lax.broadcasted_iota(jnp.int32, (group_rows, experts * slot_cap), 1)
    nothing = jnp.zeros((), jnp.bfloat16)
    combine = jnp.where(
        token_grid == slot_first[:, None], gate_first[:, None], nothing
    ) + jnp.where(token_grid == slot_second[:, None], gate_second[:, None], nothing)
    mixed = jnp.dot(combine, returned, preferred_element_type=jnp.float32).astype(jnp.bfloat16)
    prob_sum = jnp.sum(probs, axis=0)
    statistics = jnp.stack([prob_sum, first_load], axis=0)
    all_tokens = group_rows * owner_count * column_count
    totals = lax.psum(statistics, ("expert", "dp"))
    aux_loss = experts * jnp.sum(totals[0] / all_tokens * (totals[1] / all_tokens))
    return (mixed, aux_loss)


def solution(mesh):
    placed = (
        P(("expert", "dp"), None),
        P(("expert", "dp"), None),
        P(("expert", "dp"), None),
        P(),
        P(("expert", "dp"), None, None),
        P(("expert", "dp"), None, None),
    )
    return jax.shard_map(
        shards,
        mesh=mesh,
        in_specs=placed,
        out_specs=(P(("expert", "dp"), None), P()),
        check_vma=False,
    )
```

profile of v0, /device:TPU:0, one launch (start us, length us, event | category | flops | bytes accessed | tf_op | source)
XLA Modules:
  0.0 359.2 jit_solution(15551242178874864396)
XLA Ops:
  0.6 0.0 copy-start
  0.6 0.8 fusion.38
  1.4 1.0 fusion.10
  2.5 0.0 copy-done
  2.5 1.3 fusion.39
  3.9 0.1 divide_reduce_fusion
  4.0 1.0 fusion.11
  5.0 1.3 convolution_convert_fusion
  6.3 0.6 copy.14
  6.9 52.2 %all_to_all.20 = bf16[8,4,32,2048]{3,2,0,1:T(8,128)(2,1)S(1)} all-to-all(bf16[8,4,32,2048]{3,2,0,1:T(8,128)(2,1)S(1)} %copy.14), channel_id=1, replica_groups=mesh['expert'=8,'dp'=4] {'dp'}, dimensions={1} | all-to-all | bytes 8388608 | tf_op jit(solution)/shard_map/all_to_all | solution.py:8
  59.1 0.6 copy.15
  59.7 0.0 copy-start.2
  59.7 98.9 %all_to_all.21 = bf16[8,4,32,2048]{3,2,1,0:T(8,128)(2,1)S(1)} all-to-all(bf16[8,4,32,2048]{3,2,1,0:T(8,128)(2,1)S(1)} %copy.15), channel_id=1, replica_groups=mesh['expert'=8,'dp'=4] {'expert'}, dimensions={0} | all-to-all | bytes 8388608 | tf_op jit(solution)/shard_map/all_to_all | solution.py:9
  158.6 0.0 copy-done.2
  158.6 0.0 copy-start.3
  158.6 4.7 %maximum_convert_fusion = bf16[1024,1024]{1,0:T(8,128)(2,1)S(1)} fusion(bf16[1024,2048]{1,0:T(8,128)(2,1)S(1)} %bitcast.31, bf16[1,2048,1024]{2,1,0:T(8,128)(2,1)S(1)} %copy-done.2), kind=kOutput, calls=%fused_computation.4 | convolution fusion | flops 4297064448 | bytes 10485760 | tf_op jit(solution)/shard_map/dot_general | solution.py:60
  163.3 0.0 copy-done.3
  163.3 4.8 %fusion.4 = bf16[1024,2048]{1,0:T(8,128)(2,1)S(1)} fusion(bf16[1024,1024]{1,0:T(8,128)(2,1)S(1)} %maximum_convert_fusion, bf16[1,2048,1024]{2,1,0:T(8,128)(2,1)S(1)} %copy-done.3), kind=kOutput, calls=%fused_computation.6 | convolution fusion | flops 4297064448 | bytes 10485760 | tf_op jit(solution)/shard_map/dot_general | solution.py:63
  168.1 96.2 %all_to_all.22 = bf16[8,4,32,2048]{3,2,1,0:T(8,128)(2,1)S(1)} all-to-all(bf16[8,4,32,2048]{3,2,1,0:T(8,128)(2,1)S(1)} %bitcast.32), channel_id=1, replica_groups=mesh['expert'=8,'dp'=4] {'expert'}, dimensions={0} | all-to-all | bytes 8388608 | tf_op jit(solution)/shard_map/all_to_all | solution.py:14
  264.2 2.3 copy.16
  266.5 0.0 copy-start.1
  266.5 5.0 %all-to-all-start.3 = ((bf16[8,4,32,2048]{3,2,0,1:T(8,128)(2,1)}), bf16[8,4,32,2048]{3,2,0,1:T(8,128)(2,1)}, u32[]{:S(2)}, u32[]{:S(2)}) async-start(bf16[8,4,32,2048]{3,2,0,1:T(8,128)(2,1)} %copy.16), calls=%async_computation.3 | async-start | bytes 8388608 | tf_op jit(solution)/shard_map/all_to_all | solution.py:15
  271.6 80.2 %psum.7 = f32[2,32]{1,0:T(2,128)S(1)} all-reduce(f32[2,32]{1,0:T(2,128)S(1)} %pad_maximum_fusion), channel_id=1, replica_groups=mesh['expert'=8,'dp'=4] {'expert','dp'}, use_global_device_ids=true, to_apply=%region_8.9 | all-reduce | flops 64 | bytes 512 | tf_op jit(solution)/shard_map/psum | solution.py:77
  351.8 0.6 multiply_reduce_fusion
  353.0 0.0 copy-done.1
  353.1 0.0 all-to-all-done.3
  353.1 2.5 copy.17
  355.6 2.4 convolution_convert_fusion.1
  (7 shorter events, 0.1 us)
Async XLA Ops:
  0.6 1.8 copy-start
  59.7 98.9 %copy-start.2 = (bf16[1,2048,1024]{2,1,0:T(8,128)(2,1)S(1)}, bf16[1,2048,1024]{2,1,0:T(8,128)(2,1)}, u32[]{:S(2)}) copy-start(bf16[1,2048,1024]{2,1,0:T(8,128)(2,1)} %param.10) | copy-start | bytes 12582916
  158.6 4.7 %copy-start.3 = (bf16[1,2048,1024]{2,1,0:T(8,128)(2,1)S(1)}, bf16[1,2048,1024]{2,1,0:T(8,128)(2,1)}, u32[]{:S(2)}) copy-start(bf16[1,2048,1024]{2,1,0:T(8,128)(2,1)} %param.11) | copy-start | bytes 12582916
  266.5 86.5 %copy-start.1 = (s32[256,2]{0,1:T(2,128)S(1)}, s32[256,2]{0,1:T(2,128)}, u32[]{:S(2)}) copy-start(s32[256,2]{0,1:T(2,128)} %param.7) | copy-start | bytes 6148
  266.5 86.5 %all-to-all-start.3 = ((bf16[8,4,32,2048]{3,2,0,1:T(8,128)(2,1)}), bf16[8,4,32,2048]{3,2,0,1:T(8,128)(2,1)}, u32[]{:S(2)}, u32[]{:S(2)}) async-start(bf16[8,4,32,2048]{3,2,0,1:T(8,128)(2,1)} %copy.16), calls=%async_computation.3 | async-start | bytes 8388608 | tf_op jit(solution)/shard_map/all_to_all | solution.py:15
where the time goes:
time: 360 us; the launch traced here: 359 us
  blocking collectives  327 us (91%)
  matrix products  16.6 us (5%)
  local copies, waits for them, and re-layouts  6.74 us (2%)
  starting transfers between devices  4.99 us (1%)
    all_to_all x1, blocking collectives, send_rows(): lax.all_to_all(column, 'expert', split_axis=0, concat_axis=0, tiled=True)  98.9 us
    all_to_all x1, blocking collectives, return_rows(): lax.all_to_all(produced, 'expert', split_axis=0, concat_axis=0, tiled=True)  96.2 us
    psum x1, blocking collectives, shards(): totals = lax.psum(statistics, ('expert', 'dp'))  80.2 us
    all_to_all x1, blocking collectives, send_rows(): lax.all_to_all(outgoing, 'dp', split_axis=1, concat_axis=1, tiled=True)  52.2 us
  transfers between devices with their start and end apart: 1, of which 0 were waited for; matrix products, arithmetic and copies ran while one was open for 0% of the time, Pallas kernels for 0%

commit v1 on v0

--- a/solution.py
+++ b/solution.py
@@ -74,7 +74,7 @@
     prob_sum = jnp.sum(probs, axis=0)
     statistics = jnp.stack([prob_sum, first_load], axis=0)
     all_tokens = group_rows * owner_count * column_count
-    totals = lax.psum(statistics, ("expert", "dp"))
+    totals = lax.psum(lax.psum(statistics, "dp"), "expert")
     aux_loss = experts * jnp.sum(totals[0] / all_tokens * (totals[1] / all_tokens))
     return (mixed, aux_loss)
 

time: 360 us -> 348 us (0.967)
  blocking collectives: 327 us -> 316 us
    psum x1 -> x2, blocking collectives: 80.2 us -> 68.8 us  [shards(): totals = lax.psum(lax.psum(statistics, 'dp'), 'expert')]
where the time goes in v1:
time: 348 us
  blocking collectives  316 us (91%)
  matrix products  16.6 us (5%)
  local copies, waits for them, and re-layouts  6.74 us (2%)
  starting transfers between devices  4.99 us (1%)
    all_to_all x1, blocking collectives, send_rows(): lax.all_to_all(column, 'expert', split_axis=0, concat_axis=0, tiled=True)  98.9 us
    all_to_all x1, blocking collectives, return_rows(): lax.all_to_all(produced, 'expert', split_axis=0, concat_axis=0, tiled=True)  96.2 us
    psum x2, blocking collectives, shards(): totals = lax.psum(lax.psum(statistics, 'dp'), 'expert')  68.8 us
    all_to_all x1, blocking collectives, send_rows(): lax.all_to_all(outgoing, 'dp', split_axis=1, concat_axis=1, tiled=True)  52.2 us
  transfers between devices with their start and end apart: 1, of which 0 were waited for; matrix products, arithmetic and copies ran while one was open for 0% of the time, Pallas kernels for 0%

profile of v1, /device:TPU:0, one launch (start us, length us, event | category | flops | bytes accessed | tf_op | source)
XLA Modules:
  0.0 347.8 jit_solution(9459706262804889092)
XLA Ops:
  0.6 0.0 copy-start
  0.6 0.8 fusion.38
  1.4 1.0 fusion.10
  2.5 0.0 copy-done
  2.5 1.3 fusion.39
  3.9 0.1 divide_reduce_fusion
  4.0 1.0 fusion.11
  5.0 1.3 convolution_convert_fusion
  6.3 0.6 copy.14
  6.9 52.2 %all_to_all.20 = bf16[8,4,32,2048]{3,2,0,1:T(8,128)(2,1)S(1)} all-to-all(bf16[8,4,32,2048]{3,2,0,1:T(8,128)(2,1)S(1)} %copy.14), channel_id=1, replica_groups=mesh['expert'=8,'dp'=4] {'dp'}, dimensions={1} | all-to-all | bytes 8388608 | tf_op jit(solution)/shard_map/all_to_all | solution.py:8
  59.1 0.6 copy.15
  59.7 0.0 copy-start.2
  59.7 98.9 %all_to_all.21 = bf16[8,4,32,2048]{3,2,1,0:T(8,128)(2,1)S(1)} all-to-all(bf16[8,4,32,2048]{3,2,1,0:T(8,128)(2,1)S(1)} %copy.15), channel_id=1, replica_groups=mesh['expert'=8,'dp'=4] {'expert'}, dimensions={0} | all-to-all | bytes 8388608 | tf_op jit(solution)/shard_map/all_to_all | solution.py:9
  158.6 0.0 copy-done.2
  158.6 0.0 copy-start.3
  158.6 4.7 %maximum_convert_fusion = bf16[1024,1024]{1,0:T(8,128)(2,1)S(1)} fusion(bf16[1024,2048]{1,0:T(8,128)(2,1)S(1)} %bitcast.31, bf16[1,2048,1024]{2,1,0:T(8,128)(2,1)S(1)} %copy-done.2), kind=kOutput, calls=%fused_computation.4 | convolution fusion | flops 4297064448 | bytes 10485760 | tf_op jit(solution)/shard_map/dot_general | solution.py:60
  163.3 0.0 copy-done.3
  163.3 4.8 %fusion.4 = bf16[1024,2048]{1,0:T(8,128)(2,1)S(1)} fusion(bf16[1024,1024]{1,0:T(8,128)(2,1)S(1)} %maximum_convert_fusion, bf16[1,2048,1024]{2,1,0:T(8,128)(2,1)S(1)} %copy-done.3), kind=kOutput, calls=%fused_computation.6 | convolution fusion | flops 4297064448 | bytes 10485760 | tf_op jit(solution)/shard_map/dot_general | solution.py:63
  168.1 96.2 %all_to_all.22 = bf16[8,4,32,2048]{3,2,1,0:T(8,128)(2,1)S(1)} all-to-all(bf16[8,4,32,2048]{3,2,1,0:T(8,128)(2,1)S(1)} %bitcast.32), channel_id=1, replica_groups=mesh['expert'=8,'dp'=4] {'expert'}, dimensions={0} | all-to-all | bytes 8388608 | tf_op jit(solution)/shard_map/all_to_all | solution.py:14
  264.2 2.3 copy.16
  266.5 0.0 copy-start.1
  266.5 5.0 %all-to-all-start.3 = ((bf16[8,4,32,2048]{3,2,0,1:T(8,128)(2,1)}), bf16[8,4,32,2048]{3,2,0,1:T(8,128)(2,1)}, u32[]{:S(2)}, u32[]{:S(2)}) async-start(bf16[8,4,32,2048]{3,2,0,1:T(8,128)(2,1)} %copy.16), calls=%async_computation.3 | async-start | bytes 8388608 | tf_op jit(solution)/shard_map/all_to_all | solution.py:15
  271.6 49.6 %psum.14 = f32[2,32]{1,0:T(2,128)S(1)} all-reduce(f32[2,32]{1,0:T(2,128)S(1)} %pad_maximum_fusion), channel_id=1, replica_groups=mesh['expert'=8,'dp'=4] {'dp'}, use_global_device_ids=true, to_apply=%region_8.9 | all-reduce | flops 64 | bytes 512 | tf_op jit(solution)/shard_map/psum | solution.py:77
  321.2 19.2 %psum.15 = f32[2,32]{1,0:T(2,128)S(1)} all-reduce(f32[2,32]{1,0:T(2,128)S(1)} %psum.14), channel_id=1, replica_groups=mesh['expert'=8,'dp'=4] {'expert'}, use_global_device_ids=true, to_apply=%region_9.10 | all-reduce | flops 64 | bytes 512 | tf_op jit(solution)/shard_map/psum | solution.py:77
  340.4 0.6 multiply_reduce_fusion
  341.7 0.0 copy-done.1
  341.7 0.0 all-to-all-done.3
  341.7 2.5 copy.17
  344.2 2.4 convolution_convert_fusion.1
  (7 shorter events, 0.1 us)
Async XLA Ops:
  0.6 1.8 copy-start
  59.7 98.9 %copy-start.2 = (bf16[1,2048,1024]{2,1,0:T(8,128)(2,1)S(1)}, bf16[1,2048,1024]{2,1,0:T(8,128)(2,1)}, u32[]{:S(2)}) copy-start(bf16[1,2048,1024]{2,1,0:T(8,128)(2,1)} %param.10) | copy-start | bytes 12582916
  158.6 4.7 %copy-start.3 = (bf16[1,2048,1024]{2,1,0:T(8,128)(2,1)S(1)}, bf16[1,2048,1024]{2,1,0:T(8,128)(2,1)}, u32[]{:S(2)}) copy-start(bf16[1,2048,1024]{2,1,0:T(8,128)(2,1)} %param.11) | copy-start | bytes 12582916
  266.5 75.1 %copy-start.1 = (s32[256,2]{0,1:T(2,128)S(1)}, s32[256,2]{0,1:T(2,128)}, u32[]{:S(2)}) copy-start(s32[256,2]{0,1:T(2,128)} %param.7) | copy-start | bytes 6148
  266.5 75.2 %all-to-all-start.3 = ((bf16[8,4,32,2048]{3,2,0,1:T(8,128)(2,1)}), bf16[8,4,32,2048]{3,2,0,1:T(8,128)(2,1)}, u32[]{:S(2)}, u32[]{:S(2)}) async-start(bf16[8,4,32,2048]{3,2,0,1:T(8,128)(2,1)} %copy.16), calls=%async_computation.3 | async-start | bytes 8388608 | tf_op jit(solution)/shard_map/all_to_all | solution.py:15
